TPU v7x, 32 devices: a whole 2x2x4 slice. The times are simulated.
32 devices in a mesh: pp: 4 (over x, core), tp: 4 (over z), dp: 2 (over y).
Axes of the slice: x: 2, y: 2, z: 4, core: 2. Of those that a mesh axis runs over, the one named last changes fastest.
Arguments:
- act_in: bfloat16 [4, 2, 128, 4096], P('pp', 'dp', 'tp'), may hold values from -6 to 6
- stash_in: bfloat16 [4, 2, 128, 4096], P('pp', 'dp', 'tp'), may hold values from -6 to 6
- grad_in: bfloat16 [4, 2, 128, 4096], P('pp', 'dp', 'tp'), may hold values from -6 to 6
- doc_ids: int32 [4, 2, 2, 128], P('pp', 'dp'), may hold values from 0 to 15, never falling along the last dimension, each value on 1 to 64 neighbouring positions
- query_weight: bfloat16 [4, 4096, 4096], P('pp', None, 'tp'), as said below
- key_weight: bfloat16 [4, 4096, 1024], P('pp', None, 'tp'), as said below
- value_weight: bfloat16 [4, 4096, 1024], P('pp', None, 'tp'), as said below
- out_weight: bfloat16 [4, 4096, 4096], P('pp', None, 'tp'), may hold values from -0.09375 to 0.09375
Outputs:
- act_out: bfloat16 [4, 2, 128, 4096], P('pp', 'dp', 'tp')
- grad_out: bfloat16 [4, 2, 128, 4096], P('pp', 'dp', 'tp')
- grad_query: float32 [4, 4096, 4096], P('pp', 'dp', 'tp')
- grad_key: float32 [4, 4096, 1024], P('pp', 'dp', 'tp')
- grad_value: float32 [4, 4096, 1024], P('pp', 'dp', 'tp')
Inputs may be any that keep to these rules, and one draw needn't show every extreme that they name: `doc_ids`: along each row of 128 positions the document numbers never fall. `query_weight`: entries of mean zero. `key_weight`: for each of the 8 key heads, its 1 stored copies (consecutive blocks of 128 columns) are equal; entries of mean zero. `value_weight`: for each of the 8 value heads, its 1 stored copies (consecutive blocks of 128 columns) are equal.
All inputs are finite; a program needn't handle non-finite values.
Results may differ from a plain program's by a relative error of at most 0.033.
Values may be sent and summed in bfloat16 or wider, within the bound.
A program may use at most 128 MiB of HBM per device.

v0:
```python
import math
import jax
import jax.numpy as jnp
from jax import lax
from jax.sharding import PartitionSpec as P

HEAD = 128
epsilon = 1e-05


def from_behind(value, axis, steps):
    count = lax.axis_size(axis)
    pairs = [(source, (source + steps) % count) for source in range(count)]
    return lax.ppermute(value, axis, pairs)


def norm_rows(token_rows):
    widened = token_rows.astype(jnp.float32)
    inverse = lax.rsqrt(jnp.mean(widened * widened, axis=-1, keepdims=True) + epsilon)
    return ((widened * inverse).astype(jnp.bfloat16), inverse)


def allowed(documents):
    length = documents.shape[0]
    position = jnp.arange(length, dtype=jnp.int32)
    return (position[None, :] <= position[:, None]) & (documents[:, None] == documents[None, :])


def project(normed, weight):
    return jnp.dot(normed, weight, preferred_element_type=jnp.float32).astype(jnp.bfloat16)


def contract_last(left_side, right_side):
    return lax.dot_general(
        left_side, right_side, (((1,), (1,)), ((), ())), preferred_element_type=jnp.float32
    )


def split_heads(queries, keys, values, kv_local):
    length = queries.shape[0]
    group_size = queries.shape[1] // (kv_local * HEAD)
    return (
        queries.reshape(length, kv_local, group_size, HEAD),
        keys.reshape(length, kv_local, HEAD),
        values.reshape(length, kv_local, HEAD),
    )


def attend_probs(query_heads, key_heads, allowed_pairs):
    scores = jnp.einsum(
        "ihgd,jhd->hgij", query_heads, key_heads, preferred_element_type=jnp.float32
    ) * (1.0 / math.sqrt(HEAD))
    scores = jnp.where(allowed_pairs, scores, -jnp.inf)
    row_max = jnp.max(scores, axis=-1, keepdims=True)
    weights = jnp.exp(scores - row_max)
    return (weights / jnp.sum(weights, axis=-1, keepdims=True)).astype(jnp.bfloat16)


def attend_back(dmixed, queries, keys, values, probs, kv_local):
    length = queries.shape[0]
    query_heads, key_heads, value_heads = split_heads(queries, keys, values, kv_local)
    dmixed_heads = dmixed.reshape(query_heads.shape)
    dprobs = jnp.einsum(
        "ihgd,jhd->hgij", dmixed_heads, value_heads, preferred_element_type=jnp.float32
    )
    weights = probs.astype(jnp.float32)
    inner = jnp.sum(weights * dprobs, axis=-1, keepdims=True)
    dscores = (weights * (dprobs - inner) * (1.0 / math.sqrt(HEAD))).astype(jnp.bfloat16)
    dqueries = jnp.einsum("hgij,jhd->ihgd", dscores, key_heads, preferred_element_type=jnp.float32)
    dkeys = jnp.einsum("hgij,ihgd->jhd", dscores, query_heads, preferred_element_type=jnp.float32)
    dvalues = jnp.einsum("hgij,ihgd->jhd", probs, dmixed_heads, preferred_element_type=jnp.float32)
    return (
        dqueries.astype(jnp.bfloat16).reshape(length, queries.shape[1]),
        dkeys.reshape(length, kv_local * HEAD),
        dvalues.reshape(length, kv_local * HEAD),
    )


def handoff(payload, offset):
    return from_behind(payload, "pp", offset)


def per_copy(left_side, right_side, copies):
    length = left_side.shape[0] // copies
    product = jnp.einsum(
        "nsd,nse->nde",
        left_side.reshape(copies, length, left_side.shape[1]),
        right_side.reshape(copies, length, right_side.shape[1]),
        preferred_element_type=jnp.float32,
    )
    kept = lax.optimization_barrier(product.astype(jnp.bfloat16))
    return jnp.sum(kept.astype(jnp.float32), axis=0)


def body(act_in, stash_in, grad_in, doc_ids, query_weight, key_weight, value_weight, out_weight):
    kv_local = key_weight.shape[2] // HEAD
    forward_rows = act_in[0, 0]
    backward_rows = stash_in[0, 0]
    grad_rows = grad_in[0, 0]
    normed_ahead, unused_inverse = norm_rows(forward_rows)
    normed_back, inverse_back = norm_rows(backward_rows)
    ahead_full, back_full, grad_full = (
        lax.all_gather(normed_ahead, "tp", axis=0, tiled=True),
        lax.all_gather(normed_back, "tp", axis=0, tiled=True),
        lax.all_gather(grad_rows, "tp", axis=0, tiled=True),
    )
    w_query = query_weight[0]
    w_key = key_weight[0]
    w_value = value_weight[0]
    w_out = out_weight[0]
    queries_ahead = project(ahead_full, w_query)
    keys_ahead = project(ahead_full, w_key)
    values_ahead = project(ahead_full, w_value)
    query_heads, key_heads, value_heads = split_heads(
        queries_ahead, keys_ahead, values_ahead, kv_local
    )
    probs_ahead = attend_probs(query_heads, key_heads, allowed(doc_ids[0, 0, 0]))
    mixed_ahead = jnp.einsum(
        "hgij,jhd->ihgd", probs_ahead, value_heads, preferred_element_type=jnp.float32
    )
    mixed_ahead = mixed_ahead.astype(jnp.bfloat16).reshape(queries_ahead.shape)
    forward_sum = contract_last(mixed_ahead, w_out)
    queries_back = project(back_full, w_query)
    keys_back = project(back_full, w_key)
    values_back = project(back_full, w_value)
    query_back_heads, key_back_heads, unused_values = split_heads(
        queries_back, keys_back, values_back, kv_local
    )
    probs_back = attend_probs(query_back_heads, key_back_heads, allowed(doc_ids[0, 0, 1]))
    dmixed = jnp.dot(grad_full, w_out, preferred_element_type=jnp.float32).astype(jnp.bfloat16)
    dqueries, dkeys, dvalues = attend_back(
        dmixed, queries_back, keys_back, values_back, probs_back, kv_local
    )
    dkey_cols = dkeys.astype(jnp.bfloat16)
    dvalue_cols = dvalues.astype(jnp.bfloat16)
    dnormed = (
        contract_last(dqueries, w_query)
        + contract_last(dkey_cols, w_key)
        + contract_last(dvalue_cols, w_value)
    )
    forward_share, backward_share = (
        lax.psum_scatter(
            forward_sum.astype(jnp.bfloat16), "tp", scatter_dimension=0, tiled=True
        ).astype(jnp.float32),
        lax.psum_scatter(
            dnormed.astype(jnp.bfloat16), "tp", scatter_dimension=0, tiled=True
        ).astype(jnp.float32),
    )
    outgoing = (forward_rows.astype(jnp.float32) + forward_share).astype(jnp.bfloat16)
    scaled = backward_rows.astype(jnp.float32) * inverse_back
    grad_back = (
        grad_rows.astype(jnp.float32)
        + inverse_back
        * (backward_share - scaled * jnp.mean(backward_share * scaled, axis=-1, keepdims=True))
    ).astype(jnp.bfloat16)
    act_out = handoff(outgoing, 1)[None, None]
    grad_out = handoff(grad_back, -1)[None, None]
    copies = lax.axis_size("dp")
    normed_cols = lax.all_to_all(back_full, "dp", split_axis=1, concat_axis=0, tiled=True)
    all_queries, all_keys, all_values = (
        lax.all_gather(dqueries, "dp", axis=0, tiled=True),
        lax.all_gather(dkey_cols, "dp", axis=0, tiled=True),
        lax.all_gather(dvalue_cols, "dp", axis=0, tiled=True),
    )
    grad_query = per_copy(normed_cols, all_queries, copies)[None]
    grad_key = per_copy(normed_cols, all_keys, copies)[None]
    grad_value = per_copy(normed_cols, all_values, copies)[None]
    return (act_out, grad_out, grad_query, grad_key, grad_value)


def solution(mesh):
    placed = (
        P("pp", "dp", "tp", None),
        P("pp", "dp", "tp", None),
        P("pp", "dp", "tp", None),
        P("pp", "dp", None, None),
        P("pp", None, "tp"),
        P("pp", None, "tp"),
        P("pp", None, "tp"),
        P("pp", None, "tp"),
    )
    return jax.shard_map(
        body,
        mesh=mesh,
        in_specs=placed,
        out_specs=(
            P("pp", "dp", "tp", None),
            P("pp", "dp", "tp", None),
            P("pp", "dp", "tp"),
            P("pp", "dp", "tp"),
            P("pp", "dp", "tp"),
        ),
        check_vma=False,
    )
```

profile of v0, /device:TPU:1, one launch (start us, length us, event | category | flops | bytes accessed | tf_op | source)
XLA Modules:
  0.0 207.6 jit_solution(1931874249272098279)
XLA Ops:
  7.2 1.2 fusion.81
  9.1 1.8 fusion.76
  11.7 1.1 fusion.82
  12.8 1.8 fusion.83
  15.4 25.2 %all-gather.7.cloned.1.call-done = bf16[128,4096]{1,0:T(8,128)(2,1)} async-done(((bf16[32,4096]{1,0:T(8,128)(2,1)}), bf16[128,4096]{1,0:T(8,128)(2,1)}) %all-gather.7.cloned.1.call-update) | async-done | bytes 1048592 | tf_op jit(solution)/shard_map/all_gather | solution.py:104
  40.6 5.0 %fusion.42 = bf16[128,1024]{1,0:T(8,128)(2,1)S(1)} fusion(bf16[128,4096]{1,0:T(8,128)(2,1)} %all-gather.7.cloned.1.call-done, bf16[1,4096,1024]{2,1,0:T(8,128)(2,1)} %param.12), kind=kOutput, calls=%fused_computation.49 | convolution fusion | flops 1073872896 | bytes 9699328 | tf_op jit(solution)/shard_map/dot_general | solution.py:30
  45.6 0.8 copy.52
  47.1 2.0 fusion.51
  49.2 20.4 %all-gather.9.cloned.1.call-done = bf16[1,1,128,4096]{3,2,1,0:T(8,128)(2,1)} async-done(((bf16[1,1,32,4096]{3,2,1,0:T(8,128)(2,1)}), bf16[1,1,128,4096]{3,2,1,0:T(8,128)(2,1)}) %all-gather.9.cloned.1.call-update) | async-done | bytes 1048592 | tf_op jit(solution)/shard_map/all_gather | solution.py:105
  69.6 5.7 %fusion.45 = bf16[128,1024]{1,0:T(8,128)(2,1)} fusion(bf16[1,4096,1024]{2,1,0:T(8,128)(2,1)} %param.15, bf16[1,1,128,4096]{3,2,1,0:T(8,128)(2,1)} %all-gather.9.cloned.1.call-done), kind=kOutput, calls=%fused_computation.50 | convolution fusion | flops 1073872896 | bytes 9699328 | tf_op jit(solution)/shard_map/dot_general | solution.py:130
  75.3 1.1 copy.53
  76.4 2.7 %fusion.111 = (f32[2,4,128]{2,1,0:T(4,128)}, f32[2,4,128,128]{2,3,1,0:T(8,128)}) fusion(bf16[128,2,128,1]{0,2,3,1:T(8,128)(2,1)S(1)} %copy.36, bf16[128,2,4,128]{0,3,2,1:T(8,128)(2,1)} %bitcast.170, pred[128,128]{0,1:T(8,128)(4,1)} %fusion.90), kind=kOutput, calls=%fused_computation.113 | convolution fusion | flops 34078848 | bytes 872448 | tf_op jit(solution)/shard_map/sub | solution.py:55
  79.1 1.8 divide_convert_fusion
  80.9 1.0 convolution_bitcast_fusion
  81.9 2.5 %convolution_convert_fusion.3 = bf16[2,128,4,128]{3,1,2,0:T(8,128)(2,1)} fusion(bf16[128,2,128,1]{0,2,3,1:T(8,128)(2,1)S(1)} %copy.36, f32[2,4,128,128]{2,3,1,0:T(8,128)} %convolution_bitcast_fusion, bf16[2,4,128,128]{2,3,1,0:T(8,128)(2,1)} %divide_convert_fusion), kind=kOutput, calls=%fused_computation.51 | convolution fusion | flops 34604160 | bytes 1114112 | tf_op jit(solution)/shard_map/hgij,jhd->ihgd/dot_general | solution.py:69
  84.4 2.4 %fusion.60 = bf16[2,128,128]{2,1,0:T(8,128)(2,1)} fusion(bf16[128,2,4,128]{0,3,2,1:T(8,128)(2,1)} %bitcast.171, f32[2,4,128,128]{2,3,1,0:T(8,128)} %convolution_bitcast_fusion, bf16[2,4,128,128]{2,3,1,0:T(8,128)(2,1)} %divide_convert_fusion), kind=kOutput, calls=%fused_computation.59 | convolution fusion | flops 34505856 | bytes 1114112 | tf_op jit(solution)/shard_map/hgij,ihgd->jhd/dot_general | solution.py:70
  86.9 9.4 %all_gather.21 = bf16[256,1024]{0,1:T(8,128)(2,1)} all-gather(bf16[128,1024]{0,1:T(8,128)(2,1)} %bitcast.161), channel_id=1, replica_groups=mesh['pp'=4,'tp'=4,'dp'=2] {'dp'}, dimensions={0}, use_global_device_ids=true | all-gather | bytes 786432 | tf_op jit(solution)/shard_map/all_gather | solution.py:161
  96.2 2.0 copy.28
  98.3 1.3 copy.51
  99.6 3.6 %all-to-all-start = ((bf16[128,2,2048]{0,2,1:T(8,128)(2,1)}), bf16[128,2,2048]{0,2,1:T(8,128)(2,1)S(1)}, u32[]{:S(2)}, u32[]{:S(2)}) async-start(bf16[128,2,2048]{0,2,1:T(8,128)(2,1)} %bitcast.155), calls=%async_computation.2 | async-start | bytes 2097152 | tf_op jit(solution)/shard_map/all_to_all | solution.py:159
  103.2 13.3 %all_gather.22 = bf16[256,256]{0,1:T(8,128)(2,1)S(1)} all-gather(bf16[128,256]{0,1:T(8,128)(2,1)} %bitcast.167), channel_id=1, replica_groups=mesh['pp'=4,'tp'=4,'dp'=2] {'dp'}, dimensions={0}, use_global_device_ids=true | all-gather | bytes 196608 | tf_op jit(solution)/shard_map/all_gather | solution.py:162
  116.5 0.8 copy.29
  117.3 1.2 fusion.61
  118.5 3.8 %all_gather.23 = bf16[256,256]{0,1:T(8,128)(2,1)S(1)} all-gather(bf16[128,256]{0,1:T(8,128)(2,1)S(1)} %bitcast.163), channel_id=1, replica_groups=mesh['pp'=4,'tp'=4,'dp'=2] {'dp'}, dimensions={0}, use_global_device_ids=true | all-gather | bytes 196608 | tf_op jit(solution)/shard_map/all_gather | solution.py:163
  122.3 0.8 copy.30
  123.0 6.4 %fusion.7 = f32[128,4096]{1,0:T(8,128)S(1)} fusion(bf16[128,1024]{0,1:T(8,128)(2,1)} %bitcast.162, bf16[1,4096,1024]{2,1,0:T(8,128)(2,1)} %param.12), kind=kOutput, calls=%fused_computation.8 | convolution fusion | flops 1073741824 | bytes 10747904 | tf_op jit(solution)/shard_map/dot_general | solution.py:34
  129.5 0.8 convolution_add_fusion.1
  131.1 1.8 fusion.13
  133.2 5.0 %fusion.39 = bf16[128,1024]{1,0:T(8,128)(2,1)S(1)} fusion(bf16[128,4096]{1,0:T(8,128)(2,1)} %all-gather.5.cloned.1.call-done, bf16[1,4096,1024]{2,1,0:T(8,128)(2,1)} %param.12), kind=kOutput, calls=%fused_computation.48 | convolution fusion | flops 1073872896 | bytes 9699328 | tf_op jit(solution)/shard_map/dot_general | solution.py:30
  138.1 0.9 reshape.96
  139.0 1.7 fusion.54
  140.7 2.6 %fusion.48 = bf16[128,256]{1,0:T(8,128)(2,1)S(1)} fusion(bf16[128,4096]{1,0:T(8,128)(2,1)} %all-gather.5.cloned.1.call-done, bf16[1,4096,256]{2,1,0:T(8,128)(2,1)} %param.14), kind=kOutput, calls=%fused_computation.55 | convolution fusion | flops 268468224 | bytes 3211264 | tf_op jit(solution)/shard_map/dot_general | solution.py:30
  144.0 0.9 fusion.106
  144.9 1.0 fusion.37
  146.0 1.5 convolution_convert_fusion.4
  147.5 7.3 %fusion.14 = bf16[128,4096]{1,0:T(8,128)(2,1)} fusion(bf16[128,1024]{0,1:T(8,128)(2,1)S(1)} %bitcast.169, bf16[1,4096,1024]{2,1,0:T(8,128)(2,1)} %param.15), kind=kOutput, calls=%fused_computation.18 | convolution fusion | flops 1074266112 | bytes 9699328 | tf_op jit(solution)/shard_map/dot_general | solution.py:34
  154.9 6.6 %convolution_convert_fusion = bf16[2,2048,1024]{2,1,0:T(8,128)(2,1)} fusion(bf16[2,128,1024]{2,1,0:T(8,128)(2,1)} %bitcast.158, bf16[128,2,2048]{0,2,1:T(8,128)(2,1)S(1)} %all-to-all-done), kind=kOutput, calls=%fused_computation.14 | convolution fusion | flops 1077936128 | bytes 9961472 | tf_op jit(solution)/shard_map/nsd,nse->nde/dot_general | solution.py:85
  161.5 2.0 convolution_convert_fusion.2
  163.5 2.1 %convolution_convert_fusion.1 = bf16[2,2048,256]{2,1,0:T(8,128)(2,1)} fusion(bf16[2,128,256]{2,1,0:T(8,128)(2,1)S(1)} %bitcast.166, bf16[128,2,2048]{0,2,1:T(8,128)(2,1)S(1)} %all-to-all-done), kind=kOutput, calls=%fused_computation.21 | convolution fusion | flops 269484032 | bytes 3276800 | tf_op jit(solution)/shard_map/nsd,nse->nde/dot_general | solution.py:85
  165.6 10.0 %convert_reduce_fusion = f32[2048,1024]{1,0:T(8,128)} fusion(bf16[2,2048,1024]{2,1,0:T(8,128)(2,1)} %convolution_convert_fusion), kind=kLoop, calls=%fused_computation.3 | loop fusion | flops 6291456 | bytes 16777216 | tf_op jit(solution)/shard_map/reduce_sum | solution.py:92
  175.6 1.2 fusion.80
  176.9 1.2 fusion.79
  178.0 3.9 %collective-permute-start.1 = (bf16[32,4096]{1,0:T(8,128)(2,1)S(1)}, bf16[32,4096]{1,0:T(8,128)(2,1)S(1)}, u32[]{:S(2)}, u32[]{:S(2)}) collective-permute-start(bf16[32,4096]{1,0:T(8,128)(2,1)S(1)} %fusion.79), channel_id=1, source_target_pairs={{0,24},{8,0},{16,8},{24,16},{1,25},{9,1},{17,9},{25,17},{2,26},{10... | collective-permute-start | bytes 786440 | tf_op jit(solution)/shard_map/ppermute | solution.py:14
  181.9 9.3 %reduce-scatter.3.cloned.1.call-done = bf16[32,4096]{1,0:T(8,128)(2,1)} async-done(((bf16[128,4096]{1,0:T(8,128)(2,1)}), bf16[32,4096]{1,0:T(8,128)(2,1)}) %reduce-scatter.3.cloned.1.call-update) | async-done | bytes 262160 | tf_op jit(solution)/shard_map/reduce_scatter | solution.py:142
  191.2 1.0 fusion.84
  192.2 2.2 %collective-permute-start = (bf16[32,4096]{1,0:T(8,128)(2,1)S(1)}, bf16[32,4096]{1,0:T(8,128)(2,1)S(1)}, u32[]{:S(2)}, u32[]{:S(2)}) collective-permute-start(bf16[32,4096]{1,0:T(8,128)(2,1)S(1)} %fusion.84), channel_id=1, source_target_pairs={{0,8},{8,16},{16,24},{24,0},{1,9},{9,17},{17,25},{25,1},{2,10},{10... | collective-permute-start | bytes 786440 | tf_op jit(solution)/shard_map/ppermute | solution.py:14
  194.4 3.5 %convert_reduce_fusion.2 = f32[2048,256]{1,0:T(8,128)} fusion(bf16[2,2048,256]{2,1,0:T(8,128)(2,1)} %convolution_convert_fusion.2), kind=kLoop, calls=%fused_computation.20 | loop fusion | flops 1572864 | bytes 4194304 | tf_op jit(solution)/shard_map/reduce_sum | solution.py:92
  197.9 1.7 convert_reduce_fusion.1
  (59 shorter events, 6.1 us)
Async XLA Ops:
  7.2 39.3 %copy-start = (bf16[1,4096,256]{2,1,0:T(8,128)(2,1)S(1)}, bf16[1,4096,256]{2,1,0:T(8,128)(2,1)}, u32[]{:S(2)}) copy-start(bf16[1,4096,256]{2,1,0:T(8,128)(2,1)} %param.13) | copy-start | bytes 6291460
  7.2 7.4 %copy-start.14 = (s32[1,1,2,128]{3,2,1,0:T(2,128)S(1)}, s32[1,1,2,128]{3,2,1,0:T(2,128)}, u32[]{:S(2)}) copy-start(s32[1,1,2,128]{3,2,1,0:T(2,128)} %param.11) | copy-start | bytes 3076
  7.2 33.4 %all-gather.7.cloned.1.call-start = ((), (), s32[]{:S(2)}) async-start(), calls=%async_computation.5 | async-start | bytes 1310720 | tf_op jit(solution)/shard_map/all_gather | solution.py:104
  8.5 0.6 copy-start.12
  10.9 58.7 %all-gather.9.cloned.1.call-start = ((), (), s32[]{:S(2)}) async-start(), calls=%async_computation.7 | async-start | bytes 1310720 | tf_op jit(solution)/shard_map/all_gather | solution.py:105
  11.6 121.5 %all-gather.5.cloned.1.call-start = ((), (), s32[]{:S(2)}) async-start(), calls=%async_computation.3 | async-start | bytes 1310720 | tf_op jit(solution)/shard_map/all_gather | solution.py:103
  40.6 5.9 %copy-start.1 = (bf16[128,4096]{1,0:T(8,128)(2,1)S(1)}, bf16[128,4096]{1,0:T(8,128)(2,1)}, u32[]{:S(2)}) copy-start(bf16[128,4096]{1,0:T(8,128)(2,1)} %all-gather.7.cloned.1.call-done) | copy-start | bytes 3145732
  99.6 55.3 %all-to-all-start = ((bf16[128,2,2048]{0,2,1:T(8,128)(2,1)}), bf16[128,2,2048]{0,2,1:T(8,128)(2,1)S(1)}, u32[]{:S(2)}, u32[]{:S(2)}) async-start(bf16[128,2,2048]{0,2,1:T(8,128)(2,1)} %bitcast.155), calls=%async_computation.2 | async-start | bytes 2097152 | tf_op jit(solution)/shard_map/all_to_all | solution.py:159
  103.2 72.5 %reduce-scatter.5.cloned.1.call-start = ((), (), s32[]{:S(2)}) async-start(), calls=%async_computation.6 | async-start | bytes 1310720 | tf_op jit(solution)/shard_map/reduce_scatter | solution.py:145
  123.0 6.4 %copy-start.10 = (bf16[2,128,128]{2,1,0:T(8,128)(2,1)S(1)}, bf16[2,128,128]{2,1,0:T(8,128)(2,1)}, u32[]{:S(2)}) copy-start(bf16[2,128,128]{2,1,0:T(8,128)(2,1)} %fusion.60) | copy-start | bytes 196612
  129.5 1.6 copy-start.2
  132.9 58.3 %reduce-scatter.3.cloned.1.call-start = ((), (), s32[]{:S(2)}) async-start(), calls=%async_computation.4 | async-start | bytes 1310720 | tf_op jit(solution)/shard_map/reduce_scatter | solution.py:142
  140.7 3.3 %copy-start.7 = (bf16[128,2,4,128]{3,2,1,0:T(4,128)(2,1)S(1)}, bf16[128,2,4,128]{3,2,1,0:T(4,128)(2,1)}, u32[]{:S(2)}) copy-start(bf16[128,2,4,128]{3,2,1,0:T(4,128)(2,1)} %reshape.96) | copy-start | bytes 786436
  144.0 2.0 copy-start.11
  154.8 6.6 %copy-start.8 = (bf16[256,256]{1,0:T(8,128)(2,1)S(1)}, bf16[256,256]{1,0:T(8,128)(2,1)}, u32[]{:S(2)}) copy-start(bf16[256,256]{1,0:T(8,128)(2,1)} %copy.29) | copy-start | bytes 393220
  161.5 2.0 copy-start.9
  165.6 10.0 %copy-start.4 = (bf16[1,1,32,4096]{3,2,1,0:T(8,128)(2,1)S(1)}, bf16[1,1,32,4096]{3,2,1,0:T(8,128)(2,1)}, u32[]{:S(2)}) copy-start(bf16[1,1,32,4096]{3,2,1,0:T(8,128)(2,1)} %param.9) | copy-start | bytes 786436
  165.6 10.0 %copy-start.13 = (f32[32]{0:T(128)S(1)}, f32[32]{0:T(128)}, u32[]{:S(2)}) copy-start(f32[32]{0:T(128)} %copy-done.12) | copy-start | bytes 388
  165.6 11.3 %copy-start.6 = (bf16[1,1,32,4096]{3,2,1,0:T(8,128)(2,1)S(1)}, bf16[1,1,32,4096]{3,2,1,0:T(8,128)(2,1)}, u32[]{:S(2)}) copy-start(bf16[1,1,32,4096]{3,2,1,0:T(8,128)(2,1)} %param.10) | copy-start | bytes 786436
  165.6 25.6 %copy-start.5 = (bf16[1,1,32,4096]{3,2,1,0:T(8,128)(2,1)S(1)}, bf16[1,1,32,4096]{3,2,1,0:T(8,128)(2,1)}, u32[]{:S(2)}) copy-start(bf16[1,1,32,4096]{3,2,1,0:T(8,128)(2,1)} %param.8) | copy-start | bytes 786436
  178.0 21.6 %collective-permute-start.1 = (bf16[32,4096]{1,0:T(8,128)(2,1)S(1)}, bf16[32,4096]{1,0:T(8,128)(2,1)S(1)}, u32[]{:S(2)}, u32[]{:S(2)}) collective-permute-start(bf16[32,4096]{1,0:T(8,128)(2,1)S(1)} %fusion.79), channel_id=1, source_target_pairs={{0,24},{8,0},{16,8},{24,16},{1,25},{9,1},{17,9},{25,17},{2,26},{10... | collective-permute-start | bytes 786440 | tf_op jit(solution)/shard_map/ppermute | solution.py:14
  192.2 5.7 %copy-start.3 = (bf16[2,2048,256]{2,1,0:T(8,128)(2,1)S(1)}, bf16[2,2048,256]{2,1,0:T(8,128)(2,1)}, u32[]{:S(2)}) copy-start(bf16[2,2048,256]{2,1,0:T(8,128)(2,1)} %convolution_convert_fusion.1) | copy-start | bytes 6291460
  192.2 7.4 %collective-permute-start = (bf16[32,4096]{1,0:T(8,128)(2,1)S(1)}, bf16[32,4096]{1,0:T(8,128)(2,1)S(1)}, u32[]{:S(2)}, u32[]{:S(2)}) collective-permute-start(bf16[32,4096]{1,0:T(8,128)(2,1)S(1)} %fusion.84), channel_id=1, source_target_pairs={{0,8},{8,16},{16,24},{24,0},{1,9},{9,17},{17,25},{25,1},{2,10},{10... | collective-permute-start | bytes 786440 | tf_op jit(solution)/shard_map/ppermute | solution.py:14
Sparse Core Ops, SparseCore 0:
  11.0 29.5 all-gather.6
  42.2 27.4 all-gather.8
  71.8 27.2 all-gather.4
  133.0 29.5 reduce-scatter.4
  165.4 25.7 reduce-scatter.2
where the time goes:
time: 209 us; the launch traced here: 208 us
  matrix products  62.8 us (30%)
  waiting for transfers between devices  55.7 us (27%)
  other arithmetic  27.1 us (13%)
  blocking collectives  26.5 us (13%)
  between operations  14 us (7%)
  local copies, waits for them, and re-layouts  11.4 us (5%)
  starting transfers between devices  10 us (5%)
    all_gather x1, waiting for transfers between devices, body(): lax.all_gather(normed_back, 'tp', axis=0, tiled=True)  25.2 us
    all_gather x1, waiting for transfers between devices, body(): lax.all_gather(grad_rows, 'tp', axis=0, tiled=True)  20.4 us
    dot_general x6, matrix products, project(): jnp.dot(normed, weight, preferred_element_type=jnp.float32)  16.7 us
    dot_general x4, matrix products, contract_last(): lax.dot_general(left_side, right_side, (((1,), (1,)), ((), ())), preferre...  16.4 us
    reduce_sum x3, other arithmetic, per_copy(): return jnp.sum(kept.astype(jnp.float32), axis=0)  15.2 us
    all_gather x1, blocking collectives, body(): lax.all_gather(dkey_cols, 'dp', axis=0, tiled=True)  13.3 us
    dot_general x3, matrix products, per_copy(): jnp.einsum('nsd,nse->nde', left_side.reshape(copies, length, left_side.sh...  10.7 us
    all_gather x1, blocking collectives, body(): lax.all_gather(dqueries, 'dp', axis=0, tiled=True)  9.38 us
  transfers between devices with their start and end apart: 8, of which 3 were waited for; matrix products, arithmetic and copies ran while one was open for 46% of the time, Pallas kernels for 0%

commit v1 on v0

--- a/solution.py
+++ b/solution.py
@@ -6,6 +6,13 @@
 
 HEAD = 128
 epsilon = 1e-05
+
+
+def all_by_exchange(x, mesh_axis, dim):
+    count = lax.axis_size(mesh_axis)
+    tiles = jnp.stack([x for _ in range(count)])
+    tiles = lax.all_to_all(tiles, mesh_axis, split_axis=0, concat_axis=0)
+    return jnp.concatenate(tiles, axis=dim)
 
 
 def from_behind(value, axis, steps):
@@ -101,7 +108,7 @@
     normed_back, inverse_back = norm_rows(backward_rows)
     ahead_full, back_full, grad_full = (
         lax.all_gather(normed_ahead, "tp", axis=0, tiled=True),
-        lax.all_gather(normed_back, "tp", axis=0, tiled=True),
+        all_by_exchange(normed_back, "tp", 0),
         lax.all_gather(grad_rows, "tp", axis=0, tiled=True),
     )
     w_query = query_weight[0]

time: 209 us -> 213 us (1.019)
  waiting for transfers between devices: 55.7 us -> 43.6 us
  local copies, waits for them, and re-layouts: 11.4 us -> 20.6 us
  starting transfers between devices: 10 us -> 15.7 us
  matrix products: 62.8 us -> 67.5 us
  other arithmetic: 27.1 us -> 24.4 us
    all_to_all x0 -> x1, waiting for transfers between devices: none -> 40.3 us  [all_by_exchange(): tiles = lax.all_to_all(tiles, mesh_axis, split_axis=0, concat_axis=0)]
    all_gather x1 -> x0, waiting for transfers between devices: 25.2 us -> none  [body(): lax.all_gather(normed_back, 'tp', axis=0, tiled=True)]
    all_gather x1, waiting for transfers between devices: 20.4 us -> 0.02 us  [body(): lax.all_gather(grad_rows, 'tp', axis=0, tiled=True)]
    reduce_scatter x1, waiting for transfers between devices: 9.31 us -> 2.55 us  [body(): lax.psum_scatter(forward_sum.astype(jnp.bfloat16), 'tp', scatter_dimensio...]
    all_to_all x0 -> x1, starting transfers between devices: none -> 5.41 us  [all_by_exchange(): tiles = lax.all_to_all(tiles, mesh_axis, split_axis=0, concat_axis=0)]
    all_to_all x1 -> x2, local copies, waits for them, and re-layouts: 1.3 us -> 5.23 us  [body(): lax.all_to_all(back_full, 'dp', split_axis=1, concat_axis=0, tiled=True)]
  transfers between devices with their start and end apart: 8 -> 8, of which waited for: 3 -> 2; matrix products, arithmetic and copies ran while one was open for 46% -> 51% of each run, Pallas kernels for 0% -> 0%
where the time goes in v1:
time: 213 us; the launch traced here: 212 us
  matrix products  67.5 us (32%)
  waiting for transfers between devices  43.6 us (20%)
  blocking collectives  26.3 us (12%)
  other arithmetic  24.4 us (11%)
  local copies, waits for them, and re-layouts  20.6 us (10%)
  starting transfers between devices  15.7 us (7%)
  between operations  14 us (7%)
    all_to_all x1, waiting for transfers between devices, all_by_exchange(): tiles = lax.all_to_all(tiles, mesh_axis, split_axis=0, concat_axis=0)  40.3 us
    dot_general x6, matrix products, project(): jnp.dot(normed, weight, preferred_element_type=jnp.float32)  17.6 us
    dot_general x4, matrix products, contract_last(): lax.dot_general(left_side, right_side, (((1,), (1,)), ((), ())), preferre...  16.5 us
    reduce_sum x3, other arithmetic, per_copy(): return jnp.sum(kept.astype(jnp.float32), axis=0)  15.2 us
    all_gather x1, blocking collectives, body(): lax.all_gather(dkey_cols, 'dp', axis=0, tiled=True)  13.1 us
    dot_general x3, matrix products, per_copy(): jnp.einsum('nsd,nse->nde', left_side.reshape(copies, length, left_side.sh...  10.7 us
    all_gather x1, blocking collectives, body(): lax.all_gather(dqueries, 'dp', axis=0, tiled=True)  9.25 us
    ppermute x2, starting transfers between devices, from_behind(): return lax.ppermute(value, axis, pairs)  6.44 us
  transfers between devices with their start and end apart: 8, of which 2 were waited for; matrix products, arithmetic and copies ran while one was open for 51% of the time, Pallas kernels for 0%

profile of v1, /device:TPU:1, one launch (start us, length us, event | category | flops | bytes accessed | tf_op | source)
XLA Modules:
  0.0 212.1 jit_solution(9827720500313551606)
XLA Ops:
  7.9 1.2 fusion.81
  9.7 1.1 fusion.76
  10.8 1.1 stack.2
  11.8 5.4 %all-to-all-start = ((bf16[4,32,4096]{2,1,0:T(8,128)(2,1)}), bf16[4,32,4096]{2,1,0:T(8,128)(2,1)S(1)}, u32[]{:S(2)}, u32[]{:S(2)}) async-start(bf16[4,32,4096]{2,1,0:T(8,128)(2,1)} %stack.2), calls=%async_computation.1 | async-start | bytes 2097152 | tf_op jit(solution)/shard_map/all_to_all | solution.py:14
  17.4 0.8 fusion.83
  19.1 40.3 %all-to-all-done = bf16[4,32,4096]{2,1,0:T(8,128)(2,1)S(1)} async-done(((bf16[4,32,4096]{2,1,0:T(8,128)(2,1)}), bf16[4,32,4096]{2,1,0:T(8,128)(2,1)S(1)}, u32[]{:S(2)}, u32[]{:S(2)}) %all-to-all-start) | async-done | bytes 1048608 | tf_op jit(solution)/shard_map/all_to_all | solution.py:14
  59.4 5.3 %fusion.42 = bf16[128,1024]{1,0:T(8,128)(2,1)} fusion(bf16[128,4096]{1,0:T(8,128)(2,1)S(1)} %bitcast.154, bf16[1,4096,1024]{2,1,0:T(8,128)(2,1)} %param.12), kind=kOutput, calls=%fused_computation.49 | convolution fusion | flops 1073872896 | bytes 9699328 | tf_op jit(solution)/shard_map/dot_general | solution.py:37
  64.7 1.8 copy.69
  67.7 2.1 fusion.51
  69.9 5.7 %fusion.45 = bf16[128,1024]{1,0:T(8,128)(2,1)} fusion(bf16[1,4096,1024]{2,1,0:T(8,128)(2,1)} %param.15, bf16[1,1,128,4096]{3,2,1,0:T(8,128)(2,1)} %all-gather.6.cloned.1.call-done), kind=kOutput, calls=%fused_computation.50 | convolution fusion | flops 1073872896 | bytes 9699328 | tf_op jit(solution)/shard_map/dot_general | solution.py:137
  75.6 1.8 copy.70
  77.4 2.7 %fusion.111 = (f32[2,4,128]{2,1,0:T(4,128)}, f32[2,4,128,128]{2,3,1,0:T(8,128)}) fusion(bf16[128,2,128,1]{0,2,3,1:T(8,128)(2,1)S(1)} %copy-done.9, bf16[128,2,4,128]{0,3,2,1:T(8,128)(2,1)} %bitcast.172, pred[128,128]{0,1:T(8,128)(4,1)} %fusion.90), kind=kOutput, calls=%fused_computation.113 | convolution fusion | flops 34078848 | bytes 872448 | tf_op jit(solution)/shard_map/sub | solution.py:62
  80.1 1.8 divide_convert_fusion
  81.9 2.0 convolution_bitcast_fusion
  83.8 2.5 %fusion.60 = bf16[2,128,128]{2,1,0:T(8,128)(2,1)} fusion(bf16[128,2,4,128]{0,3,2,1:T(8,128)(2,1)} %bitcast.173, f32[2,4,128,128]{2,3,1,0:T(8,128)} %convolution_bitcast_fusion, bf16[2,4,128,128]{2,3,1,0:T(8,128)(2,1)} %divide_convert_fusion), kind=kOutput, calls=%fused_computation.59 | convolution fusion | flops 34505856 | bytes 1114112 | tf_op jit(solution)/shard_map/hgij,ihgd->jhd/dot_general | solution.py:77
  86.3 2.5 %convolution_convert_fusion.3 = bf16[2,128,4,128]{3,1,2,0:T(8,128)(2,1)} fusion(bf16[128,2,128,1]{0,2,3,1:T(8,128)(2,1)S(1)} %copy-done.9, f32[2,4,128,128]{2,3,1,0:T(8,128)} %convolution_bitcast_fusion, bf16[2,4,128,128]{2,3,1,0:T(8,128)(2,1)} %divide_convert_fusion), kind=kOutput, calls=%fused_computation.51 | convolution fusion | flops 34604160 | bytes 1114112 | tf_op jit(solution)/shard_map/hgij,jhd->ihgd/dot_general | solution.py:76
  88.8 9.2 %all_gather.17 = bf16[256,1024]{0,1:T(8,128)(2,1)} all-gather(bf16[128,1024]{0,1:T(8,128)(2,1)} %bitcast.163), channel_id=1, replica_groups=mesh['pp'=4,'tp'=4,'dp'=2] {'dp'}, dimensions={0}, use_global_device_ids=true | all-gather | bytes 786432 | tf_op jit(solution)/shard_map/all_gather | solution.py:168
  98.1 2.1 copy.46
  100.2 1.6 all_to_all.16
  101.7 3.7 %copy.45 = bf16[128,2,2048]{0,2,1:T(8,128)(2,1)} copy(bf16[128,2,2048]{2,1,0:T(2,128)(2,1)} %all_to_all.16) | data formatting | bytes 2097152 | tf_op jit(solution)/shard_map/all_to_all | solution.py:166
  105.4 3.6 %all-to-all-start.1 = ((bf16[128,2,2048]{0,2,1:T(8,128)(2,1)}), bf16[128,2,2048]{0,2,1:T(8,128)(2,1)S(1)}, u32[]{:S(2)}, u32[]{:S(2)}) async-start(bf16[128,2,2048]{0,2,1:T(8,128)(2,1)} %copy.45), calls=%async_computation.3 | async-start | bytes 2097152 | tf_op jit(solution)/shard_map/all_to_all | solution.py:166
  109.0 13.1 %all_gather.18 = bf16[256,256]{0,1:T(8,128)(2,1)S(1)} all-gather(bf16[128,256]{0,1:T(8,128)(2,1)} %bitcast.169), channel_id=1, replica_groups=mesh['pp'=4,'tp'=4,'dp'=2] {'dp'}, dimensions={0}, use_global_device_ids=true | all-gather | bytes 196608 | tf_op jit(solution)/shard_map/all_gather | solution.py:169
  122.9 1.2 fusion.61
  124.1 3.9 %all_gather.19 = bf16[256,256]{0,1:T(8,128)(2,1)} all-gather(bf16[128,256]{0,1:T(8,128)(2,1)S(1)} %bitcast.165), channel_id=1, replica_groups=mesh['pp'=4,'tp'=4,'dp'=2] {'dp'}, dimensions={0}, use_global_device_ids=true | all-gather | bytes 196608 | tf_op jit(solution)/shard_map/all_gather | solution.py:170
  128.1 1.7 copy.48
  129.7 6.4 %fusion.7 = f32[128,4096]{1,0:T(8,128)S(1)} fusion(bf16[128,1024]{0,1:T(8,128)(2,1)} %bitcast.164, bf16[1,4096,1024]{2,1,0:T(8,128)(2,1)} %param.12), kind=kOutput, calls=%fused_computation.8 | convolution fusion | flops 1073741824 | bytes 10747904 | tf_op jit(solution)/shard_map/dot_general | solution.py:41
  136.2 0.8 convolution_add_fusion.1
  137.8 1.8 fusion.13
  139.9 5.7 %fusion.39 = bf16[128,1024]{1,0:T(8,128)(2,1)} fusion(bf16[128,4096]{1,0:T(8,128)(2,1)} %all-gather.4.cloned.1.call-done, bf16[1,4096,1024]{2,1,0:T(8,128)(2,1)} %param.12), kind=kOutput, calls=%fused_computation.48 | convolution fusion | flops 1073872896 | bytes 9699328 | tf_op jit(solution)/shard_map/dot_general | solution.py:37
  145.5 1.8 reshape.109
  147.4 1.7 fusion.54
  149.1 2.4 %fusion.48 = bf16[128,256]{1,0:T(8,128)(2,1)S(1)} fusion(bf16[128,4096]{1,0:T(8,128)(2,1)} %all-gather.4.cloned.1.call-done, bf16[1,4096,256]{2,1,0:T(8,128)(2,1)} %param.14), kind=kOutput, calls=%fused_computation.55 | convolution fusion | flops 268468224 | bytes 3211264 | tf_op jit(solution)/shard_map/dot_general | solution.py:37
  152.2 1.9 fusion.106
  154.1 2.0 fusion.37
  156.1 2.3 %convolution_convert_fusion.4 = bf16[2,128,4,128]{3,1,2,0:T(8,128)(2,1)} fusion(bf16[128,2,128,1]{0,2,3,1:T(8,128)(2,1)S(1)} %bitcast.180, f32[2,4,128]{2,1,0:T(4,128)} %fusion.106, f32[2,4,128,128]{2,3,1,0:T(8,128)} %fusion.37), kind=kOutput, calls=%fused_computation.52 | convolution fusion | flops 34079872 | bytes 856064 | tf_op jit(solution)/shard_map/hgij,jhd->ihgd/dot_general | solution.py:125
  158.3 7.4 %fusion.14 = bf16[128,4096]{1,0:T(8,128)(2,1)} fusion(bf16[128,1024]{0,1:T(8,128)(2,1)} %bitcast.171, bf16[1,4096,1024]{2,1,0:T(8,128)(2,1)} %param.15), kind=kOutput, calls=%fused_computation.18 | convolution fusion | flops 1074266112 | bytes 9699328 | tf_op jit(solution)/shard_map/dot_general | solution.py:41
  165.8 6.6 %convolution_convert_fusion = bf16[2,2048,1024]{2,1,0:T(8,128)(2,1)} fusion(bf16[2,128,1024]{2,1,0:T(8,128)(2,1)} %bitcast.160, bf16[128,2,2048]{0,2,1:T(8,128)(2,1)S(1)} %all-to-all-done.1), kind=kOutput, calls=%fused_computation.14 | convolution fusion | flops 1077936128 | bytes 9961472 | tf_op jit(solution)/shard_map/nsd,nse->nde/dot_general | solution.py:92
  172.4 2.0 convolution_convert_fusion.2
  174.4 2.1 convolution_convert_fusion.1
  176.5 10.0 %convert_reduce_fusion = f32[2048,1024]{1,0:T(8,128)} fusion(bf16[2,2048,1024]{2,1,0:T(8,128)(2,1)} %convolution_convert_fusion), kind=kLoop, calls=%fused_computation.3 | loop fusion | flops 6291456 | bytes 16777216 | tf_op jit(solution)/shard_map/reduce_sum | solution.py:99
  186.5 1.2 fusion.80
  187.8 1.2 fusion.79
  188.9 4.3 %collective-permute-start.1 = (bf16[32,4096]{1,0:T(8,128)(2,1)S(1)}, bf16[32,4096]{1,0:T(8,128)(2,1)S(1)}, u32[]{:S(2)}, u32[]{:S(2)}) collective-permute-start(bf16[32,4096]{1,0:T(8,128)(2,1)S(1)} %fusion.79), channel_id=1, source_target_pairs={{0,24},{8,0},{16,8},{24,16},{1,25},{9,1},{17,9},{25,17},{2,26},{10... | collective-permute-start | bytes 786440 | tf_op jit(solution)/shard_map/ppermute | solution.py:21
  193.2 2.5 %reduce-scatter.3.cloned.1.call-done = bf16[32,4096]{1,0:T(8,128)(2,1)} async-done(((bf16[128,4096]{1,0:T(8,128)(2,1)}), bf16[32,4096]{1,0:T(8,128)(2,1)}) %reduce-scatter.3.cloned.1.call-update) | async-done | bytes 262160 | tf_op jit(solution)/shard_map/reduce_scatter | solution.py:149
  195.7 1.0 fusion.84
  196.8 2.2 %collective-permute-start = (bf16[32,4096]{1,0:T(8,128)(2,1)S(1)}, bf16[32,4096]{1,0:T(8,128)(2,1)S(1)}, u32[]{:S(2)}, u32[]{:S(2)}) collective-permute-start(bf16[32,4096]{1,0:T(8,128)(2,1)S(1)} %fusion.84), channel_id=1, source_target_pairs={{0,8},{8,16},{16,24},{24,0},{1,9},{9,17},{17,25},{25,1},{2,10},{10... | collective-permute-start | bytes 786440 | tf_op jit(solution)/shard_map/ppermute | solution.py:21
  199.0 3.5 %convert_reduce_fusion.2 = f32[2048,256]{1,0:T(8,128)} fusion(bf16[2,2048,256]{2,1,0:T(8,128)(2,1)} %convolution_convert_fusion.2), kind=kLoop, calls=%fused_computation.20 | loop fusion | flops 1572864 | bytes 4194304 | tf_op jit(solution)/shard_map/reduce_sum | solution.py:99
  202.4 1.7 convert_reduce_fusion.1
  (58 shorter events, 7.6 us)
Async XLA Ops:
  7.2 59.4 %copy-start = (bf16[1,4096,256]{2,1,0:T(8,128)(2,1)S(1)}, bf16[1,4096,256]{2,1,0:T(8,128)(2,1)}, u32[]{:S(2)}) copy-start(bf16[1,4096,256]{2,1,0:T(8,128)(2,1)} %param.13) | copy-start | bytes 6291460
  7.2 62.7 %all-gather.6.cloned.1.call-start = ((), (), s32[]{:S(2)}) async-start(), calls=%async_computation.7 | async-start | bytes 1310720 | tf_op jit(solution)/shard_map/all_gather | solution.py:112
  7.9 9.3 %copy-start.4 = (bf16[1,1,32,4096]{3,2,1,0:T(8,128)(2,1)S(1)}, bf16[1,1,32,4096]{3,2,1,0:T(8,128)(2,1)}, u32[]{:S(2)}) copy-start(bf16[1,1,32,4096]{3,2,1,0:T(8,128)(2,1)} %param.8) | copy-start | bytes 786436
  9.1 0.6 copy-start.11
  10.7 7.5 %copy-start.13 = (s32[1,1,2,128]{3,2,1,0:T(2,128)S(1)}, s32[1,1,2,128]{3,2,1,0:T(2,128)}, u32[]{:S(2)}) copy-start(s32[1,1,2,128]{3,2,1,0:T(2,128)} %param.11) | copy-start | bytes 3076
  11.8 47.5 %all-to-all-start = ((bf16[4,32,4096]{2,1,0:T(8,128)(2,1)}), bf16[4,32,4096]{2,1,0:T(8,128)(2,1)S(1)}, u32[]{:S(2)}, u32[]{:S(2)}) async-start(bf16[4,32,4096]{2,1,0:T(8,128)(2,1)} %stack.2), calls=%async_computation.1 | async-start | bytes 2097152 | tf_op jit(solution)/shard_map/all_to_all | solution.py:14
  17.2 122.6 %all-gather.4.cloned.1.call-start = ((), (), s32[]{:S(2)}) async-start(), calls=%async_computation.4 | async-start | bytes 1310720 | tf_op jit(solution)/shard_map/all_gather | solution.py:110
  69.9 7.5 %copy-start.9 = (bf16[128,2,128,1]{0,2,3,1:T(8,128)(2,1)S(1)}, bf16[128,2,128,1]{0,2,3,1:T(8,128)(2,1)}, u32[]{:S(2)}) copy-start(bf16[128,2,128,1]{0,2,3,1:T(8,128)(2,1)} %copy.54) | copy-start | bytes 196612
  105.4 60.4 %all-to-all-start.1 = ((bf16[128,2,2048]{0,2,1:T(8,128)(2,1)}), bf16[128,2,2048]{0,2,1:T(8,128)(2,1)S(1)}, u32[]{:S(2)}, u32[]{:S(2)}) async-start(bf16[128,2,2048]{0,2,1:T(8,128)(2,1)} %copy.45), calls=%async_computation.3 | async-start | bytes 2097152 | tf_op jit(solution)/shard_map/all_to_all | solution.py:166
  109.0 77.6 %reduce-scatter.5.cloned.1.call-start = ((), (), s32[]{:S(2)}) async-start(), calls=%async_computation.6 | async-start | bytes 1310720 | tf_op jit(solution)/shard_map/reduce_scatter | solution.py:152
  129.7 6.4 %copy-start.8 = (bf16[2,128,128]{2,1,0:T(8,128)(2,1)S(1)}, bf16[2,128,128]{2,1,0:T(8,128)(2,1)}, u32[]{:S(2)}) copy-start(bf16[2,128,128]{2,1,0:T(8,128)(2,1)} %fusion.60) | copy-start | bytes 196612
  136.2 1.6 copy-start.1
  139.6 56.1 %reduce-scatter.3.cloned.1.call-start = ((), (), s32[]{:S(2)}) async-start(), calls=%async_computation.5 | async-start | bytes 1310720 | tf_op jit(solution)/shard_map/reduce_scatter | solution.py:149
  152.2 3.9 %copy-start.10 = (bf16[128,256]{0,1:T(8,128)(2,1)S(1)}, bf16[128,256]{0,1:T(8,128)(2,1)}, u32[]{:S(2)}) copy-start(bf16[128,256]{0,1:T(8,128)(2,1)} %copy.60) | copy-start | bytes 196612
  165.8 6.6 %copy-start.6 = (bf16[256,256]{1,0:T(8,128)(2,1)S(1)}, bf16[256,256]{1,0:T(8,128)(2,1)}, u32[]{:S(2)}) copy-start(bf16[256,256]{1,0:T(8,128)(2,1)} %copy.47) | copy-start | bytes 393220
  172.4 2.0 copy-start.7
  176.5 10.0 %copy-start.3 = (bf16[1,1,32,4096]{3,2,1,0:T(8,128)(2,1)S(1)}, bf16[1,1,32,4096]{3,2,1,0:T(8,128)(2,1)}, u32[]{:S(2)}) copy-start(bf16[1,1,32,4096]{3,2,1,0:T(8,128)(2,1)} %param.9) | copy-start | bytes 786436
  176.5 10.0 %copy-start.12 = (f32[32]{0:T(128)S(1)}, f32[32]{0:T(128)}, u32[]{:S(2)}) copy-start(f32[32]{0:T(128)} %copy-done.11) | copy-start | bytes 388
  176.5 11.3 %copy-start.5 = (bf16[1,1,32,4096]{3,2,1,0:T(8,128)(2,1)S(1)}, bf16[1,1,32,4096]{3,2,1,0:T(8,128)(2,1)}, u32[]{:S(2)}) copy-start(bf16[1,1,32,4096]{3,2,1,0:T(8,128)(2,1)} %param.10) | copy-start | bytes 786436
  188.9 15.2 %collective-permute-start.1 = (bf16[32,4096]{1,0:T(8,128)(2,1)S(1)}, bf16[32,4096]{1,0:T(8,128)(2,1)S(1)}, u32[]{:S(2)}, u32[]{:S(2)}) collective-permute-start(bf16[32,4096]{1,0:T(8,128)(2,1)S(1)} %fusion.79), channel_id=1, source_target_pairs={{0,24},{8,0},{16,8},{24,16},{1,25},{9,1},{17,9},{25,17},{2,26},{10... | collective-permute-start | bytes 786440 | tf_op jit(solution)/shard_map/ppermute | solution.py:21
  196.8 5.7 %copy-start.2 = (bf16[2,2048,256]{2,1,0:T(8,128)(2,1)S(1)}, bf16[2,2048,256]{2,1,0:T(8,128)(2,1)}, u32[]{:S(2)}) copy-start(bf16[2,2048,256]{2,1,0:T(8,128)(2,1)} %convolution_convert_fusion.1) | copy-start | bytes 6291460
  196.8 7.4 %collective-permute-start = (bf16[32,4096]{1,0:T(8,128)(2,1)S(1)}, bf16[32,4096]{1,0:T(8,128)(2,1)S(1)}, u32[]{:S(2)}, u32[]{:S(2)}) collective-permute-start(bf16[32,4096]{1,0:T(8,128)(2,1)S(1)} %fusion.84), channel_id=1, source_target_pairs={{0,8},{8,16},{16,24},{24,0},{1,9},{9,17},{17,25},{25,1},{2,10},{10... | collective-permute-start | bytes 786440 | tf_op jit(solution)/shard_map/ppermute | solution.py:21
Sparse Core Ops, SparseCore 0:
  9.6 49.1 all-gather.5
  60.9 27.1 all-gather.3
  139.7 27.4 reduce-scatter.4
  169.9 25.7 reduce-scatter.2
